TPU v7x, 32 devices: a whole 2x2x4 slice. The times are simulated.
32 devices in a mesh: gx: 4 (over y, x), gy: 8 (over z, core).
Axes of the slice: x: 2, y: 2, z: 4, core: 2. Of those that a mesh axis runs over, the one named last changes fastest.
Arguments:
- velocity: float32 [2, 2048, 4096], P(None, 'gx', 'gy'), may hold values from -3 to 3
- stress: float32 [3, 2048, 4096], P(None, 'gx', 'gy'), may hold values from -3 to 3
- strength: float32 [2048, 4096], P('gx', 'gy'), may hold values from 0.5 to 4
- ice_mass: float32 [2048, 4096], P('gx', 'gy'), may hold values from 0.3 to 20, as said below
- wind_stress: float32 [2, 2048, 4096], P(None, 'gx', 'gy'), may hold values from -6 to 6
- current: float32 [2, 2048, 4096], P(None, 'gx', 'gy'), may hold values from -3 to 3
- ice_mask: int32 [2048, 4096], P('gx', 'gy'), may hold values from 0 to 1, as said below
- open_water: int32 [2048, 4096], P('gx', 'gy'), may hold values 0 or 1
Outputs:
- new_velocity: float32 [2, 2048, 4096], P(None, 'gx', 'gy')
- new_stress: float32 [3, 2048, 4096], P(None, 'gx', 'gy')
- residual: float32 [], replicated
- kinetic_energy: float32 [], replicated
Inputs may be any that keep to these rules, and one draw needn't show every extreme that they name: `ice_mask`: 1 marks an ocean cell, 0 a land cell. `ice_mass`: positive everywhere.
All inputs are finite; a program needn't handle non-finite values. No bound on the sum of `open_water` on one device may be relied on, other than what follows from the above.
Results may differ from a plain program's by a relative error of at most 0.00002.
Values sent between devices are 32-bit elements; how exact they have to be, the bound alone decides.
A program may use at most 128 MiB of HBM per device.

v0:
```python
import functools

import jax
import jax.numpy as jnp
from jax import lax
from jax.experimental import pallas as pl
from jax.experimental.pallas import tpu as pltpu
from jax.sharding import PartitionSpec as P

ITERS = 4
relax_rate = 0.8
time_step = 0.5
drag_coef = 1.0
coriolis = 0.3
delta_floor = 0.05
MESH = pl.DeviceIdType.MESH

U, V, S1, S2, S12, PR, M, TX, TY, CA, CB = range(11)
NF = 11
PAD = 8
LANE = 128
DIRS = ((-1, 0), (1, 0), (0, -1), (0, 1), (-1, -1), (-1, 1), (1, -1), (1, 1))


def exchange_kernel(
    nx, ny, rows, cols,
    vel, stress, strength, mass, wind, current, mask, water,
    dyn, par,
    strength_v, mass_v, wind_v, current_v, mask_v, water_v,
    pack_l, pack_r, recv_l, recv_r,
    load_sem, row_send, row_recv, col_send, col_recv, cor_send, cor_recv,
):
    ix = lax.axis_index("gx")
    iy = lax.axis_index("gy")
    mid = cols - 2 * LANE
    pieces = (
        (0, rows, 0, LANE),
        (0, rows, cols - LANE, LANE),
        (0, 8, LANE, mid),
        (rows - 8, 8, LANE, mid),
        (8, rows - 16, LANE, mid),
    )

    def loads(p):
        r0, nr, c0, nc = pieces[p]
        src = (pl.ds(r0, nr), pl.ds(c0, nc))
        ext = (pl.ds(r0 + PAD, nr), pl.ds(c0, nc))
        both = (slice(None),)
        pairs = (
            (strength.at[src], strength_v.at[src]),
            (mass.at[src], mass_v.at[src]),
            (mask.at[src], mask_v.at[src]),
            (water.at[src], water_v.at[src]),
            (vel.at[both + src], dyn.at[(pl.ds(U, 2),) + ext]),
            (stress.at[both + src], dyn.at[(pl.ds(S1, 3),) + ext]),
            (wind.at[both + src], wind_v.at[both + src]),
            (current.at[both + src], current_v.at[both + src]),
        )
        return [
            pltpu.make_async_copy(a, b, load_sem.at[p * 8 + k])
            for k, (a, b) in enumerate(pairs)
        ]

    for p in range(5):
        for c in loads(p):
            c.start()

    def exists(d):
        return (ix + d[0] >= 0) & (ix + d[0] < nx) & (iy + d[1] >= 0) & (iy + d[1] < ny)

    def peer(d):
        return (ix + d[0], iy + d[1])

    barrier = pltpu.get_barrier_semaphore()
    for d in DIRS:
        @pl.when(exists(d))
        def _():
            pl.semaphore_signal(barrier, inc=1, device_id=peer(d), device_id_type=MESH)
    span = jnp.minimum(ix, 1) + jnp.minimum(nx - 1 - ix, 1) + 1
    breadth = jnp.minimum(iy, 1) + jnp.minimum(ny - 1 - iy, 1) + 1
    pl.semaphore_wait(barrier, span * breadth - 1)

    def prepare(r0, nr, c0, nc, step):
        def body(k, carry):
            r = pl.multiple_of(r0 + k * step, 8)
            src = (pl.ds(r, step), pl.ds(c0, nc))
            dst = (pl.ds(pl.multiple_of(r + PAD, 8), step), pl.ds(c0, nc))
            w = mask_v[src].astype(jnp.float32) * (1.0 - water_v[src].astype(jnp.float32))
            m = mass_v[src]
            inertia = m * (1.0 / time_step)
            diagonal = inertia + drag_coef
            turning = m * coriolis
            scale = (0.25 * w) / (diagonal * diagonal + turning * turning)
            par[(PR - 5,) + dst] = strength_v[src] * w * (relax_rate / (1.0 + relax_rate))
            par[(M - 5,) + dst] = inertia * 4.0
            par[(TX - 5,) + dst] = (wind_v[(0,) + src] + drag_coef * current_v[(0,) + src]) * 4.0
            par[(TY - 5,) + dst] = (wind_v[(1,) + src] + drag_coef * current_v[(1,) + src]) * 4.0
            par[(CA - 5,) + dst] = diagonal * scale
            par[(CB - 5,) + dst] = turning * scale
            return carry

        lax.fori_loop(0, nr // step, body, 0)

    for p in range(4):
        for c in loads(p):
            c.wait()
    prepare(0, rows, 0, LANE, 32)
    prepare(0, rows, cols - LANE, LANE, 32)
    prepare(0, 8, LANE, mid, 8)
    prepare(rows - 8, 8, LANE, mid, 8)

    def plane(f):
        return (dyn, f) if f < 5 else (par, f - 5)

    lane = lax.broadcasted_iota(jnp.int32, (8, LANE), 1)
    half = rows // 2

    def pack(k, carry):
        r = pl.multiple_of(k * 8, 8)
        for out, c0, base in ((pack_l, 0, 0), (pack_r, cols - LANE, 4)):
            acc = jnp.zeros((8, LANE), jnp.float32)
            for h in range(2):
                for f in range(NF):
                    ref, q = plane(f)
                    x = ref[q, pl.ds(pl.multiple_of(r + PAD + h * half, 8), 8), pl.ds(c0, LANE)]
                    at = 4 * f + 64 * h
                    x = pltpu.roll(x, (at + base) % LANE, axis=1) if (at + base) % LANE else x
                    acc = jnp.where((lane >= at) & (lane < at + 4), x, acc)
            out[pl.ds(r, 8), :] = acc
        return carry

    lax.fori_loop(0, half // 8, pack, 0)

    def sends(d):
        dx, dy = d
        k = DIRS.index(d)
        out = []
        if dy == 0:
            a = PAD if dx < 0 else rows
            b = rows + PAD if dx < 0 else 0
            for n, ref in enumerate((dyn, par)):
                out.append((
                    ref.at[:, pl.ds(a, 8), pl.ds(0, cols)],
                    ref.at[:, pl.ds(b, 8), pl.ds(0, cols)],
                    row_send.at[2 * k + n], row_recv.at[2 * k + n],
                ))
        else:
            src, dst = (pack_l, recv_r) if dy < 0 else (pack_r, recv_l)
            if dx == 0:
                out.append((src, dst.at[pl.ds(8, half), :], col_send.at[k - 2], col_recv.at[k - 2]))
            else:
                a = 0 if dx < 0 else half - 8
                b = half + 8 if dx < 0 else 0
                out.append((
                    src.at[pl.ds(a, 8), :], dst.at[pl.ds(b, 8), :],
                    cor_send.at[k - 4], cor_recv.at[k - 4],
                ))
        return [
            pltpu.make_async_remote_copy(
                src_ref=a, dst_ref=b, send_sem=s, recv_sem=r,
                device_id=peer(d), device_id_type=MESH,
            )
            for a, b, s, r in out
        ]

    for d in DIRS:
        @pl.when(exists(d))
        def _():
            for c in sends(d):
                c.start()

    @pl.when(ix == 0)
    def _():
        for ref in (dyn, par):
            ref[:, 0:8, 0:cols] = jnp.zeros((ref.shape[0], 8, cols), jnp.float32)

    @pl.when(ix == nx - 1)
    def _():
        for ref in (dyn, par):
            ref[:, rows + PAD : rows + 16, 0:cols] = jnp.zeros((ref.shape[0], 8, cols), jnp.float32)

    for dy, buf in ((-1, recv_l), (1, recv_r)):
        @pl.when(~exists((0, dy)))
        def _():
            buf[8 : half + 8, :] = jnp.zeros((half, LANE), jnp.float32)

        for dx, b in ((-1, 0), (1, half + 8)):
            @pl.when(~exists((dx, dy)))
            def _():
                buf[b : b + 8, :] = jnp.zeros((8, LANE), jnp.float32)

    for c in loads(4):
        c.wait()
    prepare(8, rows - 16, LANE, mid, 8)

    for d in DIRS:
        @pl.when(exists(d))
        def _():
            for c in sends((-d[0], -d[1])):
                c.wait_recv()
            for c in sends(d):
                c.wait_send()

    def unpack(r, src, h):
        left = recv_l[pl.ds(src, 8), :]
        right = recv_r[pl.ds(src, 8), :]
        for f in range(NF):
            at = 4 * f + 64 * h
            x = pltpu.roll(right, LANE - at, axis=1) if at else right
            y = pltpu.roll(left, (LANE - 4 - at) % LANE, axis=1) if (LANE - 4 - at) % LANE else left
            ref, q = plane(f)
            ref[q, pl.ds(r, 8), pl.ds(cols, LANE)] = jnp.where(
                lane < 4, x, jnp.where(lane >= LANE - 4, y, 0.0)
            )

    unpack(0, 0, 1)
    unpack(rows + PAD, half + 8, 0)

    def body(k, carry):
        s = pl.multiple_of(k * 8 + 8, 8)
        for h in range(2):
            unpack(pl.multiple_of(s + h * half, 8), s, h)
        return carry

    lax.fori_loop(0, half // 8, body, 0)


def roll(x, by, axis):
    return pltpu.roll(x, by % x.shape[axis], axis=axis)


def cycle_kernel(rows, cols, dyn, par, new_vel, new_stress, part, work, acc, sem):
    wide = cols + LANE
    blocks = (rows + 2 * PAD) // 8
    keep = 1.0 / (1.0 + relax_rate)
    sub = lax.broadcasted_iota(jnp.int32, (8, wide), 0)
    first, last = sub == 0, sub == 7
    acc[...] = jnp.zeros_like(acc)

    def at(k):
        return pl.ds(pl.multiple_of(k * 8, 8), 8)

    def do_stress(src, k, q0, r0):
        u, v = src[U, at(k), :], src[V, at(k), :]
        q, r = u + v, u - v
        q1, r1 = roll(q, 1, 0), roll(r, 1, 0)
        qa, ra = jnp.where(first, q0, q1), jnp.where(first, r0, r1)
        x, y = q - ra, r - qa
        z, w = q + ra, r + qa
        d = x + roll(y, 1, 1)
        t = y + roll(x, 1, 1)
        s = z - roll(w, 1, 1)
        e = d * d + 0.25 * (t * t + s * s) + 4.0 * delta_floor * delta_floor
        pr = par[PR - 5, at(k), :]
        g = pr * lax.rsqrt(e)
        s1 = src[S1, at(k), :] * keep + (g * d - pr)
        s2 = src[S2, at(k), :] * keep + (0.25 * g) * t
        s12 = src[S12, at(k), :] * keep + (0.125 * g) * s
        work[S1, at(k), :] = s1
        work[S2, at(k), :] = s2
        work[S12, at(k), :] = s12
        return q1, r1, s1 + s2, s1 - s2, s12 + s12

    def do_vel(src, k, n, m, h, nn, mm, hh, final):
        nb, mb, hb = (
            jnp.where(last, roll(b, -1, 0), roll(a, -1, 0)) for a, b in ((n, nn), (m, mm), (h, hh))
        )
        dn, sh, dh, sm = nb - n, hb + h, hb - h, mb + m
        fx = roll(dn + sh, -1, 1) + (dn - sh)
        fy = roll(dh + sm, -1, 1) + (dh - sm)
        u, v = src[U, at(k), :], src[V, at(k), :]
        mass = par[M - 5, at(k), :]
        ru = mass * u + (fx + par[TX - 5, at(k), :])
        rv = mass * v + (fy + par[TY - 5, at(k), :])
        a, b = par[CA - 5, at(k), :], par[CB - 5, at(k), :]
        nu, nv = a * ru + b * rv, a * rv - b * ru
        work[U, at(k), :] = nu
        work[V, at(k), :] = nv
        if final:
            du, dv = (nu - u)[:, :cols], (nv - v)[:, :cols]
            acc[0] += du * du + dv * dv
            acc[1] += (mass * (nu * nu + nv * nv))[:, :cols]

    zero = jnp.zeros((8, wide), jnp.float32)

    def sweep(src, lo, hi, carry, final):
        def body(k, c):
            q0, r0, n, m, h = c
            q1, r1, nn, mm, hh = do_stress(src, k, q0, r0)
            do_vel(src, k - 1, n, m, h, nn, mm, hh, final)
            return q1, r1, nn, mm, hh

        return lax.fori_loop(lo, hi, body, carry)

    def out_copies(r0, nr, k):
        ext = (pl.ds(r0 + PAD, nr), pl.ds(0, cols))
        own = (slice(None), pl.ds(r0, nr))
        return (
            pltpu.make_async_copy(work.at[(pl.ds(U, 2),) + ext], new_vel.at[own], sem.at[2 * k]),
            pltpu.make_async_copy(work.at[(pl.ds(S1, 3),) + ext], new_stress.at[own], sem.at[2 * k + 1]),
        )

    for cyc in range(ITERS - 1):
        src = dyn if cyc == 0 else work
        carry = do_stress(src, 0, zero, zero)
        carry = sweep(src, 1, blocks, carry, False)
        q1, r1, n, m, h = carry
        do_vel(src, blocks - 1, n, m, h, n, m, h, False)

    own = rows // 8
    cuts = 4
    per = own // cuts
    _, _, n, m, h = carry = do_stress(work, 0, zero, zero)
    carry = do_stress(work, 1, carry[0], carry[1])
    for c in range(cuts):
        carry = sweep(work, 2 + c * per, 2 + (c + 1) * per, carry, True)
        for cp in out_copies(c * per * 8, per * 8, c):
            cp.start()
    part[...] = jnp.zeros_like(part)
    part[0:1, :] = sum_lanes(acc[0], cols)
    part[1:2, :] = sum_lanes(acc[1], cols)
    for c in range(cuts):
        for cp in out_copies(c * per * 8, per * 8, c):
            cp.wait()


def sum_lanes(x, cols):
    t = x[:, 0:LANE]
    for c in range(LANE, cols, LANE):
        t = t + x[:, c : c + LANE]
    return jnp.sum(t, axis=0, keepdims=True)


def sum_kernel(nx, ny, scale, part, out, slots, send_sem, recv_sem):
    n = nx * ny
    me = lax.axis_index("gx") * ny + lax.axis_index("gy")

    def target(k):
        t = lax.rem(me + k, n)
        return (t // ny, lax.rem(t, ny))

    barrier = pltpu.get_barrier_semaphore()

    def greet(k, c):
        pl.semaphore_signal(barrier, inc=1, device_id=target(k), device_id_type=MESH)
        return c

    lax.fori_loop(1, n, greet, 0)
    pl.semaphore_wait(barrier, n - 1)

    def copy(k):
        return pltpu.make_async_remote_copy(
            src_ref=part, dst_ref=slots.at[me], send_sem=send_sem.at[k], recv_sem=recv_sem.at[k],
            device_id=target(k), device_id_type=MESH,
        )

    def start(k, c):
        copy(k).start()
        return c

    lax.fori_loop(1, n, start, 0)
    slots[pl.ds(me, 1)] = part[...][None]

    def wait(k, c):
        copy(k).wait()
        return c

    lax.fori_loop(1, n, wait, 0)
    total = jnp.sum(slots[...], axis=0)
    total = jnp.sum(total, axis=1, keepdims=True)
    out[...] = jnp.broadcast_to(total * scale, out.shape)


def per_device(nx, ny, velocity, stress, strength, ice_mass, wind, current, ice_mask, open_water):
    _, rows, cols = velocity.shape
    wide, tall, half = cols + LANE, rows + 2 * PAD, rows // 2
    f32, i32 = jnp.float32, jnp.int32
    hbm = pl.BlockSpec(memory_space=pl.ANY)
    vmem = pl.BlockSpec(memory_space=pltpu.VMEM)
    dma = pltpu.SemaphoreType.DMA
    dyn, par = pl.pallas_call(
        functools.partial(exchange_kernel, nx, ny, rows, cols),
        out_shape=(
            pltpu.VMEM((5, tall, wide), f32),
            pltpu.VMEM((6, tall, wide), f32),
        ),
        in_specs=[pl.BlockSpec(memory_space=pltpu.HBM)] * 8,
        out_specs=(vmem, vmem),
        scratch_shapes=[
            pltpu.VMEM((rows, cols), f32),
            pltpu.VMEM((rows, cols), f32),
            pltpu.VMEM((2, rows, cols), f32),
            pltpu.VMEM((2, rows, cols), f32),
            pltpu.VMEM((rows, cols), i32),
            pltpu.VMEM((rows, cols), i32),
            pltpu.VMEM((half, LANE), f32),
            pltpu.VMEM((half, LANE), f32),
            pltpu.VMEM((half + 16, LANE), f32),
            pltpu.VMEM((half + 16, LANE), f32),
            dma((40,)), dma((4,)), dma((4,)), dma((2,)), dma((2,)), dma((4,)), dma((4,)),
        ],
        compiler_params=pltpu.CompilerParams(
            collective_id=0, has_side_effects=True, vmem_limit_bytes=K1_VMEM
        ),
        name="exchange",
    )(
        *[
            pltpu.with_memory_space_constraint(x, pltpu.HBM)
            for x in (velocity, stress, strength, ice_mass, wind, current, ice_mask, open_water)
        ]
    )
    new_vel, new_stress, part = pl.pallas_call(
        functools.partial(cycle_kernel, rows, cols),
        out_shape=(
            jax.ShapeDtypeStruct(velocity.shape, f32),
            jax.ShapeDtypeStruct(stress.shape, f32),
            jax.ShapeDtypeStruct((8, LANE), f32),
        ),
        in_specs=[vmem, vmem],
        out_specs=(hbm, hbm, vmem),
        scratch_shapes=[
            pltpu.VMEM((5, tall, wide), f32),
            pltpu.VMEM((2, 8, cols), f32),
            dma((8,)),
        ],
        compiler_params=pltpu.CompilerParams(vmem_limit_bytes=K2_VMEM),
        name="subcycles",
    )(dyn, par)
    sums = pl.pallas_call(
        functools.partial(sum_kernel, nx, ny, 1.0 / (rows * nx * cols * ny)),
        out_shape=jax.ShapeDtypeStruct((8, LANE), f32),
        in_specs=[vmem],
        out_specs=vmem,
        scratch_shapes=[
            pltpu.VMEM((nx * ny, 8, LANE), f32),
            dma((nx * ny,)),
            dma((nx * ny,)),
        ],
        compiler_params=pltpu.CompilerParams(
            collective_id=1, has_side_effects=True, vmem_limit_bytes=4 << 20
        ),
        name="totals",
    )(part)
    return new_vel, new_stress, sums[0, 0], sums[1, 0] * 0.0625


K1_VMEM = 12 << 20
K2_VMEM = 12 << 20


def solution(mesh):
    two, three = P("gx", "gy"), P(None, "gx", "gy")
    return jax.shard_map(
        functools.partial(per_device, mesh.shape["gx"], mesh.shape["gy"]),
        mesh=mesh,
        in_specs=(three, three, two, two, three, three, two, two),
        out_specs=(three, three, P(), P()),
        check_vma=False,
    )
```

profile of v0, /device:TPU:0, one launch (start us, length us, event | category | flops | bytes accessed | tf_op | source)
XLA Modules:
  0.0 89.9 jit_solution(4906206596014667992)
XLA Ops:
  0.6 22.6 %exchange.1 = (f32[5,528,640]{2,1,0:T(8,128)S(1)}, f32[6,528,640]{2,1,0:T(8,128)S(1)}) custom-call(f32[2,512,512]{2,1,0:T(8,128)} %vel.1, f32[3,512,512]{2,1,0:T(8,128)} %stress.1, f32[512,512]{1,0:T(8,128)} %strength.1, f32[512,512]{1,0:T(8,128)} %mass.1, f32[2,512,512]{2,1,0:T(8,128)} %wind.1, f32[2,512,512]{2,1,0:T(8,128)} %current.1, s32[512,512]{1,0:T(8,128)} %mask.1, ...), custom_call_target="tpu_custom_call" | custom-call | tf_op jit(solution)/shard_map/exchange/pallas_call | solution.py:381
  23.2 52.9 %subcycles.1 = (f32[2,512,512]{2,1,0:T(8,128)}, f32[3,512,512]{2,1,0:T(8,128)}, f32[8,128]{1,0:T(8,128)S(1)}) custom-call(f32[5,528,640]{2,1,0:T(8,128)S(1)} %get-tuple-element.9.dyn, f32[6,528,640]{2,1,0:T(8,128)S(1)} %get-tuple-element.10.par), custom_call_target="tpu_custom_call" | custom-call | tf_op jit(solution)/shard_map/subcycles/pallas_call | solution.py:412
  76.1 11.5 %totals.1 = f32[8,128]{1,0:T(8,128)S(1)} custom-call(f32[8,128]{1,0:T(8,128)S(1)} %get-tuple-element.13.part), custom_call_target="tpu_custom_call" | custom-call | tf_op jit(solution)/shard_map/totals/pallas_call | solution.py:429
  87.6 0.5 fusion
where the time goes:
time: 90.1 us; the launch traced here: 89.9 us
  Pallas kernels  86.9 us (96%)
  between operations  2.43 us (3%)
    pallas_call x1, Pallas kernels, per_device(): pl.pallas_call(functools.partial(cycle_kernel, rows, cols), out_shape=(ja...  52.9 us
    pallas_call x1, Pallas kernels, per_device(): pl.pallas_call(functools.partial(exchange_kernel, nx, ny, rows, cols), ou...  22.6 us
    pallas_call x1, Pallas kernels, per_device(): pl.pallas_call(functools.partial(sum_kernel, nx, ny, 1.0 / (rows * nx * c...  11.5 us

commit v1 on v0

--- a/solution.py
+++ b/solution.py
@@ -129,7 +129,6 @@
             out[pl.ds(r, 8), :] = acc
         return carry
 
-    lax.fori_loop(0, half // 8, pack, 0)
 
     def sends(d):
         dx, dy = d
@@ -163,7 +162,15 @@
             for a, b, s, r in out
         ]
 
-    for d in DIRS:
+    for d in DIRS[:2]:
+        @pl.when(exists(d))
+        def _():
+            for c in sends(d):
+                c.start()
+
+    lax.fori_loop(0, half // 8, pack, 0)
+
+    for d in DIRS[2:]:
         @pl.when(exists(d))
         def _():
             for c in sends(d):
@@ -229,7 +236,9 @@
     return pltpu.roll(x, by % x.shape[axis], axis=axis)
 
 
-def cycle_kernel(rows, cols, dyn, par, new_vel, new_stress, part, work, acc, sem):
+def cycle_kernel(
+    rows, cols, dyn, par, new_vel, new_stress, part, vel_a, sig_a, vel_b, sig_b, acc, sem
+):
     wide = cols + LANE
     blocks = (rows + 2 * PAD) // 8
     keep = 1.0 / (1.0 + relax_rate)
@@ -240,85 +249,102 @@
     def at(k):
         return pl.ds(pl.multiple_of(k * 8, 8), 8)
 
-    def do_stress(src, k, q0, r0):
-        u, v = src[U, at(k), :], src[V, at(k), :]
-        q, r = u + v, u - v
-        q1, r1 = roll(q, 1, 0), roll(r, 1, 0)
-        qa, ra = jnp.where(first, q0, q1), jnp.where(first, r0, r1)
-        x, y = q - ra, r - qa
-        z, w = q + ra, r + qa
-        d = x + roll(y, 1, 1)
-        t = y + roll(x, 1, 1)
-        s = z - roll(w, 1, 1)
-        e = d * d + 0.25 * (t * t + s * s) + 4.0 * delta_floor * delta_floor
-        pr = par[PR - 5, at(k), :]
-        g = pr * lax.rsqrt(e)
-        s1 = src[S1, at(k), :] * keep + (g * d - pr)
-        s2 = src[S2, at(k), :] * keep + (0.25 * g) * t
-        s12 = src[S12, at(k), :] * keep + (0.125 * g) * s
-        work[S1, at(k), :] = s1
-        work[S2, at(k), :] = s2
-        work[S12, at(k), :] = s12
-        return q1, r1, s1 + s2, s1 - s2, s12 + s12
-
-    def do_vel(src, k, n, m, h, nn, mm, hh, final):
-        nb, mb, hb = (
-            jnp.where(last, roll(b, -1, 0), roll(a, -1, 0)) for a, b in ((n, nn), (m, mm), (h, hh))
-        )
-        dn, sh, dh, sm = nb - n, hb + h, hb - h, mb + m
-        fx = roll(dn + sh, -1, 1) + (dn - sh)
-        fy = roll(dh + sm, -1, 1) + (dh - sm)
-        u, v = src[U, at(k), :], src[V, at(k), :]
-        mass = par[M - 5, at(k), :]
-        ru = mass * u + (fx + par[TX - 5, at(k), :])
-        rv = mass * v + (fy + par[TY - 5, at(k), :])
-        a, b = par[CA - 5, at(k), :], par[CB - 5, at(k), :]
-        nu, nv = a * ru + b * rv, a * rv - b * ru
-        work[U, at(k), :] = nu
-        work[V, at(k), :] = nv
-        if final:
-            du, dv = (nu - u)[:, :cols], (nv - v)[:, :cols]
-            acc[0] += du * du + dv * dv
-            acc[1] += (mass * (nu * nu + nv * nv))[:, :cols]
-
-    zero = jnp.zeros((8, wide), jnp.float32)
-
-    def sweep(src, lo, hi, carry, final):
-        def body(k, c):
-            q0, r0, n, m, h = c
-            q1, r1, nn, mm, hh = do_stress(src, k, q0, r0)
-            do_vel(src, k - 1, n, m, h, nn, mm, hh, final)
-            return q1, r1, nn, mm, hh
-
-        return lax.fori_loop(lo, hi, body, carry)
+    def sum_diff(vel, k):
+        u, v = vel[0, at(k), :], vel[1, at(k), :]
+        return u + v, u - v
+
+    def do_stress(vel, sig, to, k, count):
+        q, r = sum_diff(vel, jnp.maximum(k - 1, 0))
+        q0, r0 = roll(q, 1, 0), roll(r, 1, 0)
+        for i in range(count):
+            here = at(k + i)
+            q, r = sum_diff(vel, k + i)
+            q1, r1 = roll(q, 1, 0), roll(r, 1, 0)
+            qa, ra = jnp.where(first, q0, q1), jnp.where(first, r0, r1)
+            q0, r0 = q1, r1
+            x, y = q - ra, r - qa
+            z, w = q + ra, r + qa
+            d = x + roll(y, 1, 1)
+            t = y + roll(x, 1, 1)
+            s = z - roll(w, 1, 1)
+            e = d * d + 0.25 * (t * t + s * s) + 4.0 * delta_floor * delta_floor
+            pr = par[PR - 5, here, :]
+            g = pr * lax.rsqrt(e)
+            to[0, here, :] = sig[0, here, :] * keep + (g * d - pr)
+            to[1, here, :] = sig[1, here, :] * keep + (0.25 * g) * t
+            to[2, here, :] = sig[2, here, :] * keep + (0.125 * g) * s
+
+    def normals(sig, k):
+        s1, s2, s12 = sig[0, at(k), :], sig[1, at(k), :], sig[2, at(k), :]
+        out = s1 + s2, s1 - s2, s12 + s12
+        return out, [roll(x, -1, 0) for x in out]
+
+    def do_vel(vel, sig, to, k, count, final):
+        now, up = normals(sig, k)
+        for i in range(count):
+            here = at(k + i)
+            later, up_later = normals(sig, jnp.minimum(k + i + 1, blocks - 1))
+            n, m, h = now
+            nb, mb, hb = (jnp.where(last, b, a) for a, b in zip(up, up_later))
+            now, up = later, up_later
+            dn, sh, dh, sm = nb - n, hb + h, hb - h, mb + m
+            fx = roll(dn + sh, -1, 1) + (dn - sh)
+            fy = roll(dh + sm, -1, 1) + (dh - sm)
+            u, v = vel[0, here, :], vel[1, here, :]
+            mass = par[M - 5, here, :]
+            ru = mass * u + (fx + par[TX - 5, here, :])
+            rv = mass * v + (fy + par[TY - 5, here, :])
+            a, b = par[CA - 5, here, :], par[CB - 5, here, :]
+            nu, nv = a * ru + b * rv, a * rv - b * ru
+            to[0, here, :] = nu
+            to[1, here, :] = nv
+            if final:
+                du, dv = (nu - u)[:, :cols], (nv - v)[:, :cols]
+                acc[2 * i] += du * du + dv * dv
+                acc[2 * i + 1] += (mass * (nu * nu + nv * nv))[:, :cols]
+
+    def sweep(old, new, skip, lo, hi, final):
+        def body(p, c):
+            do_vel(old[0], new[1], new[0], 2 * (p - 2) + skip, 2, final)
+            do_stress(old[0], old[1], new[1], 2 * p + skip, 2)
+            return c
+
+        lax.fori_loop(lo, hi, body, 0)
 
     def out_copies(r0, nr, k):
-        ext = (pl.ds(r0 + PAD, nr), pl.ds(0, cols))
+        ext = (slice(None), pl.ds(r0 + PAD, nr), pl.ds(0, cols))
         own = (slice(None), pl.ds(r0, nr))
         return (
-            pltpu.make_async_copy(work.at[(pl.ds(U, 2),) + ext], new_vel.at[own], sem.at[2 * k]),
-            pltpu.make_async_copy(work.at[(pl.ds(S1, 3),) + ext], new_stress.at[own], sem.at[2 * k + 1]),
+            pltpu.make_async_copy(new[0].at[ext], new_vel.at[own], sem.at[2 * k]),
+            pltpu.make_async_copy(new[1].at[ext], new_stress.at[own], sem.at[2 * k + 1]),
         )
 
+    start = (dyn.at[0:2], dyn.at[2:5])
+    bufs = ((vel_a, sig_a), (vel_b, sig_b))
+    pairs = blocks // 2
     for cyc in range(ITERS - 1):
-        src = dyn if cyc == 0 else work
-        carry = do_stress(src, 0, zero, zero)
-        carry = sweep(src, 1, blocks, carry, False)
-        q1, r1, n, m, h = carry
-        do_vel(src, blocks - 1, n, m, h, n, m, h, False)
-
-    own = rows // 8
+        old = start if cyc == 0 else bufs[(cyc - 1) % 2]
+        new = bufs[cyc % 2]
+        do_stress(*old, new[1], 0, 4)
+        sweep(old, new, 0, 2, pairs, False)
+        do_vel(old[0], new[1], new[0], blocks - 4, 4, False)
+
+    old, new = bufs[(ITERS - 2) % 2], bufs[(ITERS - 1) % 2]
     cuts = 4
-    per = own // cuts
-    _, _, n, m, h = carry = do_stress(work, 0, zero, zero)
-    carry = do_stress(work, 1, carry[0], carry[1])
+    per = (blocks - 2) // cuts
+    do_stress(*old, new[1], 1, 4)
     for c in range(cuts):
-        carry = sweep(work, 2 + c * per, 2 + (c + 1) * per, carry, True)
+        end = c == cuts - 1
+        sweep(old, new, 1, 2 + c * per // 2, pairs - 1 if end else 2 + (c + 1) * per // 2, True)
+        if end:
+            do_stress(*old, new[1], blocks - 1, 1)
+            for j in (5, 3):
+                do_vel(old[0], new[1], new[0], blocks - j, 2, True)
         for cp in out_copies(c * per * 8, per * 8, c):
             cp.start()
     part[...] = jnp.zeros_like(part)
-    part[0:1, :] = sum_lanes(acc[0], cols)
-    part[1:2, :] = sum_lanes(acc[1], cols)
+    part[0:1, :] = sum_lanes(acc[0] + acc[2], cols)
+    part[1:2, :] = sum_lanes(acc[1] + acc[3], cols)
     for c in range(cuts):
         for cp in out_copies(c * per * 8, per * 8, c):
             cp.wait()
@@ -419,8 +445,11 @@
         in_specs=[vmem, vmem],
         out_specs=(hbm, hbm, vmem),
         scratch_shapes=[
-            pltpu.VMEM((5, tall, wide), f32),
-            pltpu.VMEM((2, 8, cols), f32),
+            pltpu.VMEM((2, tall, wide), f32),
+            pltpu.VMEM((3, tall, wide), f32),
+            pltpu.VMEM((2, tall, wide), f32),
+            pltpu.VMEM((3, tall, wide), f32),
+            pltpu.VMEM((4, 8, cols), f32),
             dma((8,)),
         ],
         compiler_params=pltpu.CompilerParams(vmem_limit_bytes=K2_VMEM),
@@ -445,7 +474,7 @@
 
 
 K1_VMEM = 12 << 20
-K2_VMEM = 12 << 20
+K2_VMEM = 24 << 20
 
 
 def solution(mesh):

time: 90.1 us -> 55.3 us (0.61)
  Pallas kernels: 86.9 us -> 52.2 us
    pallas_call x1, Pallas kernels: 52.9 us -> 21.9 us  [per_device(): pl.pallas_call(functools.partial(cycle_kernel, rows, cols), out_shape=(ja...]
    pallas_call x1, Pallas kernels: 22.6 us -> 18.8 us  [per_device(): pl.pallas_call(functools.partial(exchange_kernel, nx, ny, rows, cols), ou...]
where the time goes in v1:
time: 55.3 us; the launch traced here: 55.1 us
  Pallas kernels  52.2 us (94%)
  between operations  2.43 us (4%)
    pallas_call x1, Pallas kernels, per_device(): pl.pallas_call(functools.partial(cycle_kernel, rows, cols), out_shape=(ja...  21.9 us
    pallas_call x1, Pallas kernels, per_device(): pl.pallas_call(functools.partial(exchange_kernel, nx, ny, rows, cols), ou...  18.8 us
    pallas_call x1, Pallas kernels, per_device(): pl.pallas_call(functools.partial(sum_kernel, nx, ny, 1.0 / (rows * nx * c...  11.5 us

profile of v1, /device:TPU:0, one launch (start us, length us, event | category | flops | bytes accessed | tf_op | source)
XLA Modules:
  0.0 55.1 jit_solution(17293030194003426936)
XLA Ops:
  0.6 18.8 %exchange.1 = (f32[5,528,640]{2,1,0:T(8,128)S(1)}, f32[6,528,640]{2,1,0:T(8,128)S(1)}) custom-call(f32[2,512,512]{2,1,0:T(8,128)} %vel.1, f32[3,512,512]{2,1,0:T(8,128)} %stress.1, f32[512,512]{1,0:T(8,128)} %strength.1, f32[512,512]{1,0:T(8,128)} %mass.1, f32[2,512,512]{2,1,0:T(8,128)} %wind.1, f32[2,512,512]{2,1,0:T(8,128)} %current.1, s32[512,512]{1,0:T(8,128)} %mask.1, ...), custom_call_target="tpu_custom_call" | custom-call | tf_op jit(solution)/shard_map/exchange/pallas_call | solution.py:407
  19.4 21.9 %subcycles.1 = (f32[2,512,512]{2,1,0:T(8,128)}, f32[3,512,512]{2,1,0:T(8,128)}, f32[8,128]{1,0:T(8,128)S(1)}) custom-call(f32[5,528,640]{2,1,0:T(8,128)S(1)} %get-tuple-element.9.dyn, f32[6,528,640]{2,1,0:T(8,128)S(1)} %get-tuple-element.10.par), custom_call_target="tpu_custom_call" | custom-call | tf_op jit(solution)/shard_map/subcycles/pallas_call | solution.py:438
  41.3 11.5 %totals.1 = f32[8,128]{1,0:T(8,128)S(1)} custom-call(f32[8,128]{1,0:T(8,128)S(1)} %get-tuple-element.13.part), custom_call_target="tpu_custom_call" | custom-call | tf_op jit(solution)/shard_map/totals/pallas_call | solution.py:458
  52.8 0.5 fusion
